TPU v7x, 32 devices: a whole 2x2x4 slice. The times are simulated.
32 devices in a mesh: replica: 2 (over x), tp: 16 (over z, y, core).
Axes of the slice: x: 2, y: 2, z: 4, core: 2. Of those that a mesh axis runs over, the one named last changes fastest.
Arguments:
- hidden_in: bfloat16 [8, 16384], P('replica', 'tp'), parts along dimension 0, may hold values from -60 to 60
- norm_gain: bfloat16 [16384], P('tp'), may hold values from 0.5 to 1.5
- w_qkv: bfloat16 [16384, 9216], P(None, 'tp'), may hold values from -0.046875 to 0.046875
- w_out: bfloat16 [8192, 16384], P('tp'), may hold values from -0.09375 to 0.09375
- key_cache: bfloat16 [8, 2048, 512], P('replica', 'tp'), parts along dimension 0, may hold values from -1200 to 1200
- value_cache: bfloat16 [8, 2048, 512], P('replica', 'tp'), parts along dimension 0, may hold values from -6 to 6
- lengths: int32 [8], P('replica'), parts along dimension 0, may hold values from 1024 to 2048
- positions: int32 [8], P('replica'), parts along dimension 0, may hold values from 0 to 4095
Outputs:
- attn_out: bfloat16 [8, 16384], P('replica', 'tp'), parts along dimension 0
- token_scale: float32 [8], P('replica'), parts along dimension 0
There are 2 independent parts, one for each index of `replica`. A program takes and returns all parts, laid end to end along the dimension named above; an argument that names none is the same for every part. Nothing has to cross between parts.
All inputs are finite; a program needn't handle non-finite values.
Results may differ from a plain program's by a relative error of at most 0.017.
The roundings to bfloat16 on the way count: a program that leaves them out, or rounds other values in their place, can miss the bound.
Values may be sent and summed in bfloat16 or wider, within the bound.
A program may use at most 128 MiB of HBM per device.

v0:
```python
import functools

import jax
import jax.numpy as jnp
import numpy as np
from jax import lax
from jax.experimental import pallas as pl
from jax.experimental.pallas import tpu as pltpu
from jax.sharding import PartitionSpec as P

QUERY_HEADS = 64
KEY_VALUE_HEADS = 4
HEAD_SIZE = 128
LANES = 128


def rounded_up(value, step):
    return (value + step - 1) // step * step


def kernel(
    n,
    hidden_hbm,
    gain_hbm,
    wq_hbm,
    wo_hbm,
    key_hbm,
    value_hbm,
    lens_ref,
    pos_ref,
    freq_ref,
    out_ref,
    scale_ref,
    xg,
    gained,
    quant,
    wq,
    wo,
    kv,
    vv,
    stage,
    qg,
    heads,
    so,
    og,
    rs_send,
    rs_recv,
    x_local,
    g_local,
    wq_sem,
    wo_sem,
    kv_sem,
    x_send,
    x_recv,
    q_send,
    q_recv,
    o_send,
    o_recv,
    r_send,
    r_recv,
):
    me = lax.axis_index("tp")
    dx = wo.shape[2]
    batch = lens_ref.shape[0]
    pieces = dx // LANES
    x_rows = pieces * batch
    gain_at = xg.shape[1] - rounded_up(pieces, 8)
    cw, width = wq_hbm.shape
    blocks = stage.shape[0] // batch
    padded = blocks * LANES
    own_rows = og.shape[1]
    own_heads = own_rows // batch
    positions = key_hbm.shape[1]
    group = QUERY_HEADS // KEY_VALUE_HEADS
    f32, bf16 = jnp.float32, jnp.bfloat16

    def wq_copy(c):
        span = pl.ds(pl.multiple_of(c * dx, dx), dx)
        return pltpu.make_async_copy(wq_hbm.at[:, span], wq.at[:, span], wq_sem.at[c])

    def wo_copy(c):
        return pltpu.make_async_copy(
            wo_hbm.at[:, pl.ds(pl.multiple_of(c * dx, dx), dx)], wo.at[c], wo_sem.at[c]
        )

    def remote(src, dst, send, recv, peer):
        return pltpu.make_async_remote_copy(
            src_ref=src,
            dst_ref=dst,
            send_sem=send,
            recv_sem=recv,
            device_id={"tp": peer},
            device_id_type=pl.DeviceIdType.MESH,
        )

    def each_peer(act):
        def step(k, carry):
            act(lax.rem(me + k, n))
            return carry

        lax.fori_loop(1, n, step, 0)

    local_x = pltpu.make_async_copy(hidden_hbm, xg.at[me, pl.ds(0, x_rows), :], x_local)
    local_g = pltpu.make_async_copy(gain_hbm, xg.at[me, pl.ds(gain_at, pieces), :], g_local)
    local_x.start()
    local_g.start()

    barrier = pltpu.get_barrier_semaphore()
    each_peer(
        lambda peer: pl.semaphore_signal(
            barrier, inc=1, device_id={"tp": peer}, device_id_type=pl.DeviceIdType.MESH
        )
    )

    def start_wq(c, carry):
        wq_copy(c).start()
        return carry

    lax.fori_loop(0, n, start_wq, 0)
    copy_k = pltpu.make_async_copy(key_hbm, kv, kv_sem.at[0])
    copy_v = pltpu.make_async_copy(value_hbm, vv, kv_sem.at[1])
    copy_k.start()
    copy_v.start()

    def start_wo(k, carry):
        wo_copy(lax.rem(me + 1 + k, n)).start()
        return carry

    lax.fori_loop(0, n, start_wo, 0)

    local_x.wait()
    local_g.wait()
    pl.semaphore_wait(barrier, n - 1)

    def send_x(peer):
        remote(xg.at[me], xg.at[me], x_send.at[peer], x_recv.at[me], peer).start()

    each_peer(send_x)

    row4 = lax.broadcasted_iota(jnp.int32, (8, LANES), 0) % batch
    place = jnp.zeros((8, LANES), f32)
    for b in range(batch):
        place = jnp.where(row4 == b, pos_ref[b].astype(f32), place)
    angle = place * freq_ref[...]
    cosine = jnp.cos(angle)
    sine = jnp.sin(angle)
    lane8 = lax.broadcasted_iota(jnp.int32, (8, LANES), 1)
    sine = jnp.where(lane8 < HEAD_SIZE // 2, -sine, sine)

    half8 = lax.broadcasted_iota(jnp.int32, (8, LANES), 0) // batch
    per8 = 8 // batch

    def gain_piece(s, squares, peak):
        x = xg[s, 0:x_rows, :].astype(f32)
        g = xg[s, gain_at : gain_at + rounded_up(pieces, 8), :].astype(f32)
        for j in range(x_rows // 8):
            x8 = x[8 * j : 8 * j + 8, :]
            g8 = jnp.zeros((8, LANES), f32)
            for u in range(per8):
                r = j * per8 + u
                g8 = jnp.where(half8 == u, g[r : r + 1, :], g8)
            squares = squares + x8 * x8
            y = x8 * g8
            gained[s, 8 * j : 8 * j + 8, :] = y
            peak = jnp.maximum(peak, jnp.abs(y))
        return squares, peak

    zero = jnp.zeros((8, LANES), f32)
    squares, peak = gain_piece(me, zero, zero)

    def take_x(k, carry):
        s = lax.rem(me + k, n)
        remote(xg.at[s], xg.at[s], x_send.at[s], x_recv.at[s], s).wait_recv()
        return gain_piece(s, *carry)

    squares, peak = lax.fori_loop(1, n, take_x, (squares, peak))
    squares = sum(squares[u * batch : (u + 1) * batch, :] for u in range(per8))
    peak = functools.reduce(
        jnp.maximum, [peak[u * batch : (u + 1) * batch, :] for u in range(per8)]
    )
    rstd = lax.rsqrt(jnp.sum(squares, axis=-1, keepdims=True) / width + 1e-05)
    token_scale = (jnp.max(peak, axis=-1, keepdims=True) * rstd + 1e-06) / 448.0
    rstd_rows = jnp.tile(jnp.broadcast_to(rstd, (batch, LANES)), (per8, 1))
    scale_rows = jnp.tile(jnp.broadcast_to(token_scale, (batch, LANES)), (per8, 1))
    rstd_rows = jnp.tile(rstd_rows, (x_rows // 8, 1))
    scale_rows = jnp.tile(scale_rows, (x_rows // 8, 1))
    for b in range(batch):
        scale_ref[b] = jnp.max(token_scale[b : b + 1, :])

    per = 4 if n % 4 == 0 else 1

    def project(i, acc):
        for u in range(per):
            c = i * per + u
            wq_copy(c).wait()
            span = pl.ds(pl.multiple_of(c * dx, dx), dx)
            rows = gained[c] * rstd_rows / scale_rows
            quant[:, span] = jnp.concatenate(
                [rows[j * batch : (j + 1) * batch, :] for j in range(pieces)], axis=1
            ).astype(bf16)
        span = pl.ds(pl.multiple_of(i * per * dx, per * dx), per * dx)
        return acc + lax.dot_general(
            wq[:, span], quant[:, span], (((1,), (1,)), ((), ())), preferred_element_type=f32
        )

    acc = lax.fori_loop(0, n // per, project, jnp.zeros((cw, batch), f32))
    proj = (acc.T * token_scale).astype(bf16).astype(f32)
    if padded > cw:
        proj = jnp.concatenate([proj, jnp.zeros((batch, padded - cw), f32)], axis=1)
    if cw % LANES:
        proj = pltpu.roll(proj, lax.rem(me * cw, LANES), 1)
    for j in range(blocks):
        stage[j * batch : (j + 1) * batch, :] = proj[:, j * LANES : (j + 1) * LANES]
    qg[me, 0 : blocks * batch, :] = stage[...].astype(bf16)
    each_peer(
        lambda peer: remote(
            qg.at[me], qg.at[me], q_send.at[peer], q_recv.at[me], peer
        ).start()
    )
    each_peer(lambda s: remote(qg.at[s], qg.at[s], q_send.at[s], q_recv.at[s], s).wait_recv())

    total_heads = QUERY_HEADS + 2 * KEY_VALUE_HEADS
    unpacked = [qg[d].astype(f32) for d in range(n)]
    for h in range(total_heads):
        piece = None
        for d in range(h * LANES // cw, (h * LANES + LANES - 1) // cw + 1):
            block = h - d * cw // LANES
            part = unpacked[d][block * batch : (block + 1) * batch, :]
            piece = part if piece is None else piece + part
        heads[h * batch : (h + 1) * batch, :] = piece

    def rotated(rows):
        count = rows.shape[0]
        turned = pltpu.roll(rows, HEAD_SIZE // 2, 1)
        return rows * jnp.tile(cosine, (count // 8, 1)) + turned * jnp.tile(sine, (count // 8, 1))

    copy_k.wait()
    copy_v.wait()
    inv = 1.0 / HEAD_SIZE**0.5
    rows_g = group * batch
    cols = batch * positions
    col = lax.broadcasted_iota(jnp.int32, (8, cols), 1)
    row = lax.broadcasted_iota(jnp.int32, (8, cols), 0)
    limit = jnp.zeros((8, cols), jnp.int32)
    for b in range(batch):
        limit = jnp.where(col // positions == b, lens_ref[b], limit)
    valid8 = (row % batch == col // positions) & (me * positions + col % positions < limit)
    bias8 = jnp.where(valid8, 0.0, -1e30)
    bias = jnp.tile(bias8, (rows_g // 8, 1))
    valid = bias == 0.0
    fresh_rows = rotated(
        heads[QUERY_HEADS * batch : (QUERY_HEADS + KEY_VALUE_HEADS) * batch, :]
    )
    lane = lax.broadcasted_iota(jnp.int32, (rows_g, LANES), 1)
    for g in range(KEY_VALUE_HEADS):
        q = rotated(heads[g * rows_g : (g + 1) * rows_g, :]).astype(bf16)
        k_rows = kv[:, :, g * HEAD_SIZE : (g + 1) * HEAD_SIZE].reshape(cols, HEAD_SIZE)
        v_rows = vv[:, :, g * HEAD_SIZE : (g + 1) * HEAD_SIZE].reshape(cols, HEAD_SIZE)
        s = (
            lax.dot_general(q, k_rows, (((1,), (1,)), ((), ())), preferred_element_type=f32) * inv
        )
        top = jnp.max(jnp.where(valid, s, -1e30), axis=-1, keepdims=True)
        w = jnp.where(valid, jnp.exp(s - top), 0.0)
        total = jnp.sum(w, axis=-1, keepdims=True)
        o = jnp.dot(w.astype(bf16), v_rows, preferred_element_type=f32)
        k_new = fresh_rows[g * batch : (g + 1) * batch, :]
        base = (QUERY_HEADS + KEY_VALUE_HEADS + g) * batch
        v_new = heads[base : base + batch, :]
        s_new = (
            jnp.sum(q.astype(f32) * jnp.tile(k_new, (group, 1)), axis=-1, keepdims=True) * inv
        )
        s_new = jnp.where(me == 0, s_new, -1e30)
        top_new = jnp.maximum(top, s_new)
        keep = jnp.exp(top - top_new)
        fresh = jnp.where(me == 0, jnp.exp(s_new - top_new), 0.0)
        total = total * keep + fresh
        o = o * keep + fresh * jnp.tile(v_new, (group, 1))
        some = total > 0.0
        safe = jnp.where(some, total, 1.0)
        o = o / safe
        lse = jnp.where(some, top_new + jnp.log(safe), -1e30)
        hi = lse.astype(bf16).astype(f32)
        rest = lse - hi
        mid = rest.astype(bf16).astype(f32)
        low = rest - mid
        tail = jnp.where(
            lane == 0, hi, jnp.where(lane == 1, mid, jnp.where(lane == 2, low, 0.0))
        )
        both = jnp.concatenate([o, tail], axis=1).astype(bf16)
        for j in range(group // own_heads):
            so[g * (group // own_heads) + j] = both[j * own_rows : (j + 1) * own_rows, :]

    each_peer(
        lambda peer: remote(
            so.at[peer], og.at[me], o_send.at[peer], o_recv.at[me], peer
        ).start()
    )
    og[me] = so[me]
    each_peer(lambda s: remote(so.at[s], og.at[s], o_send.at[s], o_recv.at[s], s).wait_recv())

    lses = [
        jnp.sum(og[s, :, LANES : 2 * LANES].astype(f32), axis=-1, keepdims=True) for s in range(n)
    ]
    best = functools.reduce(jnp.maximum, lses)
    den = jnp.zeros_like(best)
    num = jnp.zeros((own_rows, LANES), f32)
    for s in range(n):
        share = jnp.exp(lses[s] - best)
        den = den + share
        num = num + share * og[s, :, 0:LANES].astype(f32)
    att = num / den
    att = jnp.concatenate(
        [att[j * batch : (j + 1) * batch, :] for j in range(own_heads)], axis=1
    ).astype(bf16)

    def rows_of(part):
        return jnp.concatenate(
            [part[:, j * LANES : (j + 1) * LANES] for j in range(pieces)], axis=0
        )

    unroll = 3 if (n - 1) % 3 == 0 else 1

    def project_out(i, carry):
        parts = []
        for u in range(unroll):
            e = lax.rem(me + 1 + i * unroll + u, n)
            wo_copy(e).wait()
            parts.append(jnp.dot(att, wo[e], preferred_element_type=f32))
        for u in range(unroll):
            e = lax.rem(me + 1 + i * unroll + u, n)
            rs_send[e] = rows_of(parts[u]).astype(bf16)
            remote(rs_send.at[e], rs_recv.at[me], r_send.at[e], r_recv.at[me], e).start()
        return carry

    lax.fori_loop(0, (n - 1) // unroll, project_out, 0)
    wo_copy(me).wait()
    own = rows_of(jnp.dot(att, wo[me], preferred_element_type=f32))

    def take_r(k, carry):
        s = lax.rem(me + k, n)
        remote(rs_send.at[s], rs_recv.at[s], r_send.at[s], r_recv.at[s], s).wait_recv()
        return carry + rs_recv[s].astype(f32)

    out_ref[...] = lax.fori_loop(1, n, take_r, own).astype(bf16)

    def finish(peer):
        remote(xg.at[me], xg.at[me], x_send.at[peer], x_recv.at[me], peer).wait_send()
        remote(qg.at[me], qg.at[me], q_send.at[peer], q_recv.at[me], peer).wait_send()
        remote(so.at[peer], og.at[me], o_send.at[peer], o_recv.at[me], peer).wait_send()
        remote(rs_send.at[peer], rs_recv.at[me], r_send.at[peer], r_recv.at[me], peer).wait_send()

    each_peer(finish)


def on_device(n, hidden_in, norm_gain, w_qkv, w_out, key_cache, value_cache, lengths, positions):
    batch, dx = hidden_in.shape
    cw = w_qkv.shape[1]
    own_rows = w_out.shape[0] // HEAD_SIZE * batch
    total_heads = QUERY_HEADS + 2 * KEY_VALUE_HEADS
    widest = max(d * cw % LANES for d in range(n)) + cw
    blocks = rounded_up(widest, LANES) // LANES
    pieces = dx // LANES
    x_height = rounded_up(pieces * batch, 8) + rounded_up(pieces, 8)
    half = HEAD_SIZE // 2
    freq = np.float32(500000.0) ** (
        -(np.arange(half, dtype=np.float32) * np.float32(2.0)) / np.float32(HEAD_SIZE)
    )
    freq = jnp.asarray(np.tile(freq.astype(np.float32), 2)[None, :])
    bf16, f32 = jnp.bfloat16, jnp.float32
    dma = pltpu.SemaphoreType.DMA
    hbm = pl.BlockSpec(memory_space=pl.ANY)
    smem = pl.BlockSpec(memory_space=pltpu.SMEM)
    vmem = pl.BlockSpec(memory_space=pltpu.VMEM)
    out, token_scale = pl.pallas_call(
        functools.partial(kernel, n),
        out_shape=(
            jax.ShapeDtypeStruct((pieces * batch, LANES), bf16),
            jax.ShapeDtypeStruct((batch,), f32),
        ),
        in_specs=[hbm] * 6 + [smem, smem, vmem],
        out_specs=(vmem, smem),
        scratch_shapes=[
            pltpu.VMEM((n, x_height, LANES), bf16),
            pltpu.VMEM((n, pieces * batch, LANES), f32),
            pltpu.VMEM((batch, n * dx), bf16),
            pltpu.VMEM((cw, n * dx), bf16),
            pltpu.VMEM((n, w_out.shape[0], dx), bf16),
            pltpu.VMEM(key_cache.shape, bf16),
            pltpu.VMEM(value_cache.shape, bf16),
            pltpu.VMEM((blocks * batch, LANES), f32),
            pltpu.VMEM((n, rounded_up(blocks * batch, 8), LANES), bf16),
            pltpu.VMEM((total_heads * batch, HEAD_SIZE), f32),
            pltpu.VMEM((n, own_rows, 2 * LANES), bf16),
            pltpu.VMEM((n, own_rows, 2 * LANES), bf16),
            pltpu.VMEM((n, pieces * batch, LANES), bf16),
            pltpu.VMEM((n, pieces * batch, LANES), bf16),
            dma(()),
            dma(()),
            dma((n,)),
            dma((n,)),
            dma((2,)),
        ]
        + [dma((n,))] * 8,
        compiler_params=pltpu.CompilerParams(
            collective_id=0, has_side_effects=True, vmem_limit_bytes=60 * 1024 * 1024
        ),
        name="decode",
    )(
        hidden_in.reshape(batch, pieces, LANES).transpose(1, 0, 2).reshape(-1, LANES),
        norm_gain.reshape(dx // LANES, LANES),
        w_qkv.T,
        w_out,
        key_cache,
        value_cache,
        lengths,
        positions,
        freq,
    )
    out = out.reshape(pieces, batch, LANES).transpose(1, 0, 2).reshape(batch, dx)
    return out, token_scale


def solution(mesh):
    placed = (
        P("replica", "tp"),
        P("tp"),
        P(None, "tp"),
        P("tp", None),
        P("replica", "tp", None),
        P("replica", "tp", None),
        P("replica"),
        P("replica"),
    )
    return jax.shard_map(
        functools.partial(on_device, mesh.shape["tp"]),
        mesh=mesh,
        in_specs=placed,
        out_specs=(P("replica", "tp"), P("replica")),
        check_vma=False,
    )
```

profile of v0, /device:TPU:0, one launch (start us, length us, event | category | flops | bytes accessed | tf_op | source)
XLA Modules:
  0.0 41.3 jit_solution(11083486205873715954)
XLA Ops:
  0.6 38.2 %decode.1 = (bf16[32,128]{1,0:T(8,128)(2,1)}, f32[4]{0:T(128)}) custom-call(bf16[32,128]{1,0:T(8,128)(2,1)} %bitcast.13, bf16[8,128]{1,0:T(8,128)(2,1)} %bitcast.15, bf16[576,16384]{1,0:T(8,128)(2,1)} %bitcast.12, bf16[512,16384]{1,0:T(8,128)(2,1)} %wo_hbm.1, bf16[4,128,512]{2,1,0:T(8,128)(2,1)} %key_hbm.1, bf16[4,128,512]{2,1,0:T(8,128)(2,1)} %value_hbm.1, ...), custom_call_target="tpu_custom_call" | custom-call | tf_op jit(solution)/shard_map/decode/pallas_call | solution.py:374
  38.8 1.3 %copy.15 = bf16[4,1024]{1,0:T(4,128)(2,1)} copy(bf16[4,1024]{1,0:T(4,128)(2,1)} %bitcast.14) | data formatting | bytes 16384
  40.1 1.1 %copy.16 = f32[4]{0:T(128)} copy(f32[4]{0:T(128)} %get-tuple-element.9) | data formatting | bytes 32
where the time goes:
time: 41.6 us; the launch traced here: 41.3 us
  Pallas kernels  38.2 us (92%)
  local copies, waits for them, and re-layouts  2.44 us (6%)
  between operations  0.64 us (2%)
    pallas_call x1, Pallas kernels, on_device(): pl.pallas_call(functools.partial(kernel, n), out_shape=(jax.ShapeDtypeStr...  38.2 us
    unnamed x2, local copies, waits for them, and re-layouts  2.44 us

commit v1 on v0

v1 whole, which is shorter than its diff:
```python
import functools

import jax
import jax.numpy as jnp
import numpy as np
from jax import lax
from jax.experimental import pallas as pl
from jax.experimental.pallas import tpu as pltpu
from jax.sharding import PartitionSpec as P

QUERY_HEADS = 64
KEY_VALUE_HEADS = 4
HEAD_SIZE = 128
LANES = 128


def rounded_up(value, step):
    return (value + step - 1) // step * step


def partner(me, k, n):
    peer = me
    bit = 1
    while bit < n:
        if isinstance(k, int):
            if k & bit:
                peer = peer + (bit - 2 * bit * ((me // bit) % 2))
        else:
            mine, flip = (me // bit) % 2, (k // bit) % 2
            peer = peer + bit * flip * (1 - 2 * mine)
        bit *= 2
    return peer


def kernel(
    n,
    hidden_hbm,
    gain_hbm,
    wq_hbm,
    wo_hbm,
    key_hbm,
    value_hbm,
    lens_hbm,
    pos_hbm,
    freq_hbm,
    out_ref,
    scale_ref,
    xg,
    quant,
    wq,
    wo,
    kv,
    vv,
    stats,
    stage,
    qg,
    heads,
    so,
    og,
    sl,
    lg,
    rs_send,
    rs_recv,
    lens_ref,
    pos_ref,
    freq_ref,
    local_sem,
    wq_sem,
    wo_sem,
    kv_sem,
    t_send,
    t_recv,
    x_send,
    x_recv,
    q_send,
    q_recv,
    o_send,
    o_recv,
    l_send,
    l_recv,
    r_send,
    r_recv,
):
    me = lax.axis_index("tp")
    dx = wo.shape[1] // n
    batch = lens_ref.shape[0]
    pieces = dx // LANES
    x_rows = pieces * batch
    gain_at = xg.shape[1] - rounded_up(pieces, 8)
    cw, width = wq_hbm.shape
    blocks = stage.shape[0] // batch
    padded = blocks * LANES
    own_rows = og.shape[1]
    own_heads = own_rows // batch
    positions = key_hbm.shape[1]
    group = QUERY_HEADS // KEY_VALUE_HEADS
    f32, bf16 = jnp.float32, jnp.bfloat16
    unrolled = n <= 16

    per = 4
    groups = n // per
    span_of = lambda base: pl.ds(pl.multiple_of(base * dx, per * dx), per * dx)

    def base_of(i):
        return partner(me, i * per, n) // per * per

    def wq_copy(i):
        span = span_of(base_of(i))
        return pltpu.make_async_copy(wq_hbm.at[:, span], wq.at[:, span], wq_sem.at[i])

    def wo_copy(i):
        span = span_of(base_of(i))
        return pltpu.make_async_copy(wo_hbm.at[:, span], wo.at[:, span], wo_sem.at[i])

    def remote(src, dst, send, recv, peer):
        return pltpu.make_async_remote_copy(
            src_ref=src,
            dst_ref=dst,
            send_sem=send,
            recv_sem=recv,
            device_id={"tp": peer},
            device_id_type=pl.DeviceIdType.MESH,
        )

    def far_first(act):
        if unrolled:
            for k in range(n - 1, 0, -1):
                act(k, partner(me, k, n))
        else:

            def step(i, carry):
                act(n - 1 - i, partner(me, n - 1 - i, n))
                return carry

            lax.fori_loop(0, n - 1, step, 0)

    def all_sent(ref, send, recv):
        part = ref.at[pl.ds(0, n - 1)]
        remote(part, part, send, recv, partner(me, 1, n)).wait_send()

    def all_received(ref, send, recv, count=n - 1):
        part = ref.at[pl.ds(0, count)]
        remote(part, part, send, recv, partner(me, 1, n)).wait_recv()

    small = [
        (hidden_hbm, xg.at[me, pl.ds(0, x_rows), :]),
        (gain_hbm, xg.at[me, pl.ds(gain_at, pieces), :]),
        (freq_hbm, freq_ref),
        (pos_hbm, pos_ref),
        (lens_hbm, lens_ref),
    ]
    small = [
        pltpu.make_async_copy(src, dst, local_sem.at[i]) for i, (src, dst) in enumerate(small)
    ]
    for copy in small:
        copy.start()

    barrier = pltpu.get_barrier_semaphore()
    far_first(
        lambda k, peer: pl.semaphore_signal(
            barrier, inc=1, device_id={"tp": peer}, device_id_type=pl.DeviceIdType.MESH
        )
    )
    copy_k = pltpu.make_async_copy(key_hbm, kv, kv_sem.at[0])
    copy_v = pltpu.make_async_copy(value_hbm, vv, kv_sem.at[1])

    small[0].wait()
    small[1].wait()

    half8 = lax.broadcasted_iota(jnp.int32, (8, LANES), 0) // batch
    row4 = lax.broadcasted_iota(jnp.int32, (8, LANES), 0) % batch
    lane8 = lax.broadcasted_iota(jnp.int32, (8, LANES), 1)
    per8 = 8 // batch

    def gained(s):
        x = xg[s, 0:x_rows, :].astype(f32)
        g = xg[s, gain_at : gain_at + rounded_up(pieces, 8), :].astype(f32)
        xs, ys = [], []
        for j in range(x_rows // 8):
            x8 = x[8 * j : 8 * j + 8, :]
            g8 = jnp.zeros((8, LANES), f32)
            for u in range(per8):
                r = j * per8 + u
                g8 = jnp.where(half8 == u, g[r : r + 1, :], g8)
            xs.append(x8)
            ys.append(x8 * g8)
        return xs, ys

    xs, ys = gained(me)
    squares = sum(x8 * x8 for x8 in xs)
    peak = functools.reduce(jnp.maximum, [jnp.abs(y) for y in ys])
    squares = jnp.sum(squares, axis=-1, keepdims=True)
    peak = jnp.max(peak, axis=-1, keepdims=True)
    first = jnp.sum(jnp.where(lane8 == row4, squares, 0.0), axis=0, keepdims=True)
    second = jnp.max(jnp.where(lane8 == row4 + batch, peak, 0.0), axis=0, keepdims=True)
    stats[me] = jnp.where(lane8[0:1, :] < batch, first, second)

    for i in range(groups):
        wq_copy(i).start()

    pl.semaphore_wait(barrier, n - 1)

    far_first(
        lambda k, peer: remote(stats.at[me], stats.at[me], t_send, t_recv, peer).start()
    )
    far_first(
        lambda k, peer: remote(xg.at[me], xg.at[me], x_send, x_recv.at[k // per], peer).start()
    )

    for copy in small[2:]:
        copy.wait()
    place = jnp.zeros((8, LANES), f32)
    for b in range(batch):
        place = jnp.where(row4 == b, pos_ref[b].astype(f32), place)
    angle = place * freq_ref[...]
    cosine = jnp.cos(angle)
    sine = jnp.sin(angle)
    sine = jnp.where(lane8 < HEAD_SIZE // 2, -sine, sine)

    all_received(stats, t_send, t_recv)
    if n % 8 == 0:
        rows = [stats[8 * i : 8 * i + 8, 0, :] for i in range(n // 8)]
        added = jnp.sum(sum(rows), axis=0, keepdims=True)
        largest = jnp.max(functools.reduce(jnp.maximum, rows), axis=0, keepdims=True)
    else:
        rows = [stats[i] for i in range(n)]
        added = sum(rows)
        largest = functools.reduce(jnp.maximum, rows)
    added = jnp.sum(jnp.where(lane8 == row4, added, 0.0), axis=-1, keepdims=True)
    largest = jnp.max(jnp.where(lane8 == row4 + batch, largest, 0.0), axis=-1, keepdims=True)
    rstd8 = lax.rsqrt(added / width + 1e-05)
    scale8 = (largest * rstd8 + 1e-06) / 448.0
    token_scale = scale8[0:batch, :]
    scale_ref[...] = jnp.sum(
        jnp.where((lane8 == row4) & (half8 == 0), scale8, 0.0), axis=0, keepdims=True
    )[:, 0:batch]
    rstd8 = jnp.broadcast_to(rstd8, (8, LANES))
    scale8 = jnp.broadcast_to(scale8, (8, LANES))

    copy_k.start()
    copy_v.start()
    for i in range(groups - 1, -1, -1):
        wo_copy(i).start()

    all_received(xg, x_send, x_recv.at[0], per - 1)

    def project(i, acc):
        base = base_of(i)
        wq_copy(i).wait()

        @pl.when(i > 0)
        def _():
            all_received(xg, x_send, x_recv.at[i], per)

        for u in range(per):
            _, ys = gained(base + u)
            rows = [y * rstd8 / scale8 for y in ys]
            flat = [row[v * batch : (v + 1) * batch, :] for row in rows for v in range(per8)]
            span = pl.ds(pl.multiple_of((base + u) * dx, dx), dx)
            quant[:, span] = jnp.concatenate(flat, axis=1).astype(bf16)
        span = span_of(base)
        return acc + lax.dot_general(
            wq[:, span], quant[:, span], (((1,), (1,)), ((), ())), preferred_element_type=f32
        )

    acc = lax.fori_loop(0, groups, project, jnp.zeros((cw, batch), f32))
    proj = (acc.T * token_scale).astype(bf16).astype(f32)
    if padded > cw:
        proj = jnp.concatenate([proj, jnp.zeros((batch, padded - cw), f32)], axis=1)
    if cw % LANES:
        proj = pltpu.roll(proj, lax.rem(me * cw, LANES), 1)
    for j in range(blocks):
        stage[j * batch : (j + 1) * batch, :] = proj[:, j * LANES : (j + 1) * LANES]
    qg[me, 0 : blocks * batch, :] = stage[...].astype(bf16)
    far_first(lambda k, peer: remote(qg.at[me], qg.at[me], q_send, q_recv, peer).start())
    copy_k.wait()
    copy_v.wait()
    all_received(qg, q_send, q_recv)

    total_heads = QUERY_HEADS + 2 * KEY_VALUE_HEADS
    unpacked = [qg[d].astype(f32) for d in range(n)]
    for h in range(total_heads):
        piece = None
        for d in range(h * LANES // cw, (h * LANES + LANES - 1) // cw + 1):
            block = h - d * cw // LANES
            part = unpacked[d][block * batch : (block + 1) * batch, :]
            piece = part if piece is None else piece + part
        heads[h * batch : (h + 1) * batch, :] = piece

    def rotated(rows):
        count = rows.shape[0]
        turned = pltpu.roll(rows, HEAD_SIZE // 2, 1)
        return rows * jnp.tile(cosine, (count // 8, 1)) + turned * jnp.tile(sine, (count // 8, 1))

    inv = 1.0 / HEAD_SIZE**0.5
    rows_g = group * batch
    cols = batch * positions
    col = lax.broadcasted_iota(jnp.int32, (8, cols), 1)
    row = lax.broadcasted_iota(jnp.int32, (8, cols), 0)
    limit = jnp.zeros((8, cols), jnp.int32)
    for b in range(batch):
        limit = jnp.where(col // positions == b, lens_ref[b], limit)
    valid8 = (row % batch == col // positions) & (me * positions + col % positions < limit)
    bias8 = jnp.where(valid8, 0.0, -1e30)
    bias = jnp.tile(bias8, (rows_g // 8, 1))
    valid = bias == 0.0
    fresh_rows = rotated(
        heads[QUERY_HEADS * batch : (QUERY_HEADS + KEY_VALUE_HEADS) * batch, :]
    )
    own_lane = lax.broadcasted_iota(jnp.int32, (own_rows, LANES), 1)
    own_row = lax.broadcasted_iota(jnp.int32, (own_rows, LANES), 0)
    diagonal = own_lane == own_row
    for g in range(KEY_VALUE_HEADS):
        q = rotated(heads[g * rows_g : (g + 1) * rows_g, :]).astype(bf16)
        k_rows = kv[:, :, g * HEAD_SIZE : (g + 1) * HEAD_SIZE].reshape(cols, HEAD_SIZE)
        v_rows = vv[:, :, g * HEAD_SIZE : (g + 1) * HEAD_SIZE].reshape(cols, HEAD_SIZE)
        s = (
            lax.dot_general(q, k_rows, (((1,), (1,)), ((), ())), preferred_element_type=f32) * inv
        )
        top = jnp.max(jnp.where(valid, s, -1e30), axis=-1, keepdims=True)
        w = jnp.where(valid, jnp.exp(s - top), 0.0)
        total = jnp.sum(w, axis=-1, keepdims=True)
        o = jnp.dot(w.astype(bf16), v_rows, preferred_element_type=f32)
        k_new = fresh_rows[g * batch : (g + 1) * batch, :]
        base = (QUERY_HEADS + KEY_VALUE_HEADS + g) * batch
        v_new = heads[base : base + batch, :]
        s_new = (
            jnp.sum(q.astype(f32) * jnp.tile(k_new, (group, 1)), axis=-1, keepdims=True) * inv
        )
        s_new = jnp.where(me == 0, s_new, -1e30)
        top_new = jnp.maximum(top, s_new)
        keep = jnp.exp(top - top_new)
        fresh = jnp.where(me == 0, jnp.exp(s_new - top_new), 0.0)
        total = total * keep + fresh
        o = o * keep + fresh * jnp.tile(v_new, (group, 1))
        some = total > 0.0
        safe = jnp.where(some, total, 1.0)
        o = (o / safe).astype(bf16)
        lse = jnp.where(some, top_new + jnp.log(safe), -1e30)
        for j in range(group // own_heads):
            e = g * (group // own_heads) + j
            so[e] = o[j * own_rows : (j + 1) * own_rows, :]
            sl[e] = jnp.sum(
                jnp.where(diagonal, lse[j * own_rows : (j + 1) * own_rows, :], 0.0),
                axis=0,
                keepdims=True,
            )

    def send_o(k, peer):
        remote(so.at[peer], og.at[me], o_send, o_recv, peer).start()
        remote(sl.at[peer], lg.at[me], l_send, l_recv, peer).start()

    far_first(send_o)
    og[me] = so[me]
    lg[me] = sl[me]
    for i in range(groups):
        wo_copy(i).wait()

    all_received(lg, l_send, l_recv)
    all_received(og, o_send, o_recv)

    lses = [
        jnp.sum(jnp.where(diagonal, lg[s], 0.0), axis=-1, keepdims=True) for s in range(n)
    ]
    best = functools.reduce(jnp.maximum, lses)
    den = jnp.zeros_like(best)
    num = jnp.zeros((own_rows, LANES), f32)
    for s in range(n):
        share = jnp.exp(lses[s] - best)
        den = den + share
        num = num + share * og[s].astype(f32)
    att = num / den
    att = jnp.concatenate(
        [att[j * batch : (j + 1) * batch, :] for j in range(own_heads)], axis=1
    ).astype(bf16)

    def rows_of(part):
        return jnp.concatenate(
            [part[:, j * LANES : (j + 1) * LANES] for j in range(pieces)], axis=0
        )

    def send_part(peer, part):
        rs_send[peer] = rows_of(part).astype(bf16)
        remote(rs_send.at[peer], rs_recv.at[me], r_send, r_recv, peer).start()

    def project_out(j, carry):
        i = groups - 1 - j
        base = base_of(i)
        parts = jnp.dot(att, wo[:, span_of(base)], preferred_element_type=f32)
        for u in range(per):
            send_part(base + u, parts[:, u * dx : (u + 1) * dx])
        return carry

    lax.fori_loop(0, groups - 1, project_out, 0)

    def out_of(peer):
        span = pl.ds(pl.multiple_of(peer * dx, dx), dx)
        return jnp.dot(att, wo[:, span], preferred_element_type=f32)

    near = [partner(me, k, n) for k in range(per - 1, 0, -1)]
    parts = [out_of(peer) for peer in near]
    for peer, part in zip(near, parts):
        send_part(peer, part)
    own = rows_of(out_of(me))

    all_received(rs_recv, r_send, r_recv)
    total = own
    if unrolled:
        for k in range(1, n):
            total = total + rs_recv[partner(me, k, n)].astype(f32)
    else:
        total = lax.fori_loop(
            1, n, lambda k, t: t + rs_recv[partner(me, k, n)].astype(f32), total
        )
    out_ref[...] = total.astype(bf16)

    all_sent(stats, t_send, t_recv)
    all_sent(xg, x_send, x_recv.at[0])
    all_sent(qg, q_send, q_recv)
    all_sent(so, o_send, o_recv)
    all_sent(sl, l_send, l_recv)
    all_sent(rs_send, r_send, r_recv)


def hand_over(result_ref, scale_ref, out_ref, token_scale_ref):
    out_ref[...] = result_ref[...]
    token_scale_ref[...] = scale_ref[...]


def on_device(n, hidden_in, norm_gain, w_qkv, w_out, key_cache, value_cache, lengths, positions):
    batch, dx = hidden_in.shape
    cw = w_qkv.shape[1]
    own_rows = w_out.shape[0] // HEAD_SIZE * batch
    total_heads = QUERY_HEADS + 2 * KEY_VALUE_HEADS
    widest = max(d * cw % LANES for d in range(n)) + cw
    blocks = rounded_up(widest, LANES) // LANES
    pieces = dx // LANES
    x_height = rounded_up(pieces * batch, 8) + rounded_up(pieces, 8)
    half = HEAD_SIZE // 2
    freq = np.float32(500000.0) ** (
        -(np.arange(half, dtype=np.float32) * np.float32(2.0)) / np.float32(HEAD_SIZE)
    )
    freq = jnp.asarray(np.tile(freq.astype(np.float32), 2)[None, :])
    bf16, f32 = jnp.bfloat16, jnp.float32
    dma = pltpu.SemaphoreType.DMA
    hbm = pl.BlockSpec(memory_space=pl.ANY)
    vmem = pl.BlockSpec(memory_space=pltpu.VMEM)
    out, token_scale = pl.pallas_call(
        functools.partial(kernel, n),
        out_shape=(
            jax.ShapeDtypeStruct((pieces * batch, LANES), bf16),
            jax.ShapeDtypeStruct((1, batch), f32),
        ),
        in_specs=[hbm] * 9,
        out_specs=(vmem, vmem),
        scratch_shapes=[
            pltpu.VMEM((n, x_height, LANES), bf16),
            pltpu.VMEM((batch, n * dx), bf16),
            pltpu.VMEM((cw, n * dx), bf16),
            pltpu.VMEM((w_out.shape[0], n * dx), bf16),
            pltpu.VMEM(key_cache.shape, bf16),
            pltpu.VMEM(value_cache.shape, bf16),
            pltpu.VMEM((n, 1, LANES), f32),
            pltpu.VMEM((blocks * batch, LANES), f32),
            pltpu.VMEM((n, rounded_up(blocks * batch, 8), LANES), bf16),
            pltpu.VMEM((total_heads * batch, HEAD_SIZE), f32),
            pltpu.VMEM((n, own_rows, LANES), bf16),
            pltpu.VMEM((n, own_rows, LANES), bf16),
            pltpu.VMEM((n, 1, LANES), f32),
            pltpu.VMEM((n, 1, LANES), f32),
            pltpu.VMEM((n, pieces * batch, LANES), bf16),
            pltpu.VMEM((n, pieces * batch, LANES), bf16),
            pltpu.SMEM((batch,), jnp.int32),
            pltpu.SMEM((batch,), jnp.int32),
            pltpu.VMEM((1, LANES), f32),
            dma((5,)),
            dma((n // 4,)),
            dma((n // 4,)),
            dma((2,)),
            dma(()),
            dma(()),
            dma(()),
            dma((n // 4,)),
        ]
        + [dma(())] * 8,
        compiler_params=pltpu.CompilerParams(
            collective_id=0, has_side_effects=True, vmem_limit_bytes=60 * 1024 * 1024
        ),
        name="decode",
    )(
        hidden_in.reshape(batch, pieces, LANES).transpose(1, 0, 2).reshape(-1, LANES),
        norm_gain.reshape(dx // LANES, LANES),
        w_qkv.T,
        w_out,
        key_cache,
        value_cache,
        lengths,
        positions,
        freq,
    )
    out, token_scale = pl.pallas_call(
        hand_over,
        out_shape=(
            jax.ShapeDtypeStruct(out.shape, out.dtype),
            jax.ShapeDtypeStruct(token_scale.shape, token_scale.dtype),
        ),
        in_specs=[vmem, vmem],
        out_specs=(vmem, vmem),
        name="hand_over",
    )(out, token_scale)
    out = out.reshape(pieces, batch, LANES).transpose(1, 0, 2).reshape(batch, dx)
    return out, token_scale.reshape(batch)


def solution(mesh):
    placed = (
        P("replica", "tp"),
        P("tp"),
        P(None, "tp"),
        P("tp", None),
        P("replica", "tp", None),
        P("replica", "tp", None),
        P("replica"),
        P("replica"),
    )
    return jax.shard_map(
        functools.partial(on_device, mesh.shape["tp"]),
        mesh=mesh,
        in_specs=placed,
        out_specs=(P("replica", "tp"), P("replica")),
        check_vma=False,
    )
```

time: 41.6 us -> 34.9 us (0.84)
  Pallas kernels: 38.2 us -> 33.9 us
  local copies, waits for them, and re-layouts: 2.44 us -> 0 us
    pallas_call x1, Pallas kernels: 38.2 us -> 32.6 us  [on_device(): pl.pallas_call(functools.partial(kernel, n), out_shape=(jax.ShapeDtypeStr...]
    unnamed x2 -> x0, local copies, waits for them, and re-layouts: 2.44 us -> none
    pallas_call x0 -> x1, Pallas kernels: none -> 1.3 us  [on_device(): pl.pallas_call(hand_over, out_shape=(jax.ShapeDtypeStruct(out.shape, out....]
where the time goes in v1:
time: 34.9 us; the launch traced here: 34.6 us
  Pallas kernels  33.9 us (97%)
  between operations  0.64 us (2%)
    pallas_call x1, Pallas kernels, on_device(): pl.pallas_call(functools.partial(kernel, n), out_shape=(jax.ShapeDtypeStr...  32.6 us
    pallas_call x1, Pallas kernels, on_device(): pl.pallas_call(hand_over, out_shape=(jax.ShapeDtypeStruct(out.shape, out....  1.3 us

profile of v1, /device:TPU:0, one launch (start us, length us, event | category | flops | bytes accessed | tf_op | source)
XLA Modules:
  0.0 34.6 jit_solution(6601622390584654582)
XLA Ops:
  0.6 32.6 %decode.1 = (bf16[32,128]{1,0:T(8,128)(2,1)}, f32[1,4]{1,0:T(1,128)}) custom-call(bf16[32,128]{1,0:T(8,128)(2,1)} %bitcast.14, bf16[8,128]{1,0:T(8,128)(2,1)} %bitcast.15, bf16[576,16384]{1,0:T(8,128)(2,1)} %bitcast.13, bf16[512,16384]{1,0:T(8,128)(2,1)} %wo_hbm.1, bf16[4,128,512]{2,1,0:T(8,128)(2,1)} %key_hbm.1, bf16[4,128,512]{2,1,0:T(8,128)(2,1)} %value_hbm.1, ...), custom_call_target="tpu_custom_call" | custom-call | tf_op jit(solution)/shard_map/decode/pallas_call | solution.py:448
  33.3 1.3 %hand_over.1 = (bf16[32,128]{1,0:T(8,128)(2,1)}, f32[1,4]{1,0:T(1,128)}) custom-call(bf16[32,128]{1,0:T(8,128)(2,1)} %get-tuple-element.6.result_ref, f32[1,4]{1,0:T(1,128)} %get-tuple-element.7.scale_ref), custom_call_target="tpu_custom_call" | custom-call | tf_op jit(solution)/shard_map/hand_over/pallas_call | solution.py:501

commit v2 on v1

--- a/solution.py
+++ b/solution.py
@@ -48,13 +48,15 @@
     xg,
     quant,
     wq,
+    wt,
+    wz,
     wo,
     kv,
     vv,
     stats,
-    stage,
     qg,
     heads,
+    ordered,
     so,
     og,
     sl,
@@ -88,8 +90,7 @@
     x_rows = pieces * batch
     gain_at = xg.shape[1] - rounded_up(pieces, 8)
     cw, width = wq_hbm.shape
-    blocks = stage.shape[0] // batch
-    padded = blocks * LANES
+    padded = qg.shape[2]
     own_rows = og.shape[1]
     own_heads = own_rows // batch
     positions = key_hbm.shape[1]
@@ -104,9 +105,27 @@
     def base_of(i):
         return partner(me, i * per, n) // per * per
 
+    half = per // 2
+    turned = wt.shape[1]
+
+    def half_of(i):
+        return pl.multiple_of(partner(me, i * half, n) // half * half * dx, half * dx)
+
     def wq_copy(i):
-        span = span_of(base_of(i))
+        span = pl.ds(half_of(i), half * dx)
         return pltpu.make_async_copy(wq_hbm.at[:, span], wq.at[:, span], wq_sem.at[i])
+
+    def turn_into(ref, i, place):
+        start = half_of(i)
+        for j in range(half * dx // LANES):
+            at = pl.multiple_of(start + j * LANES, LANES)
+            to = pl.multiple_of(place * half * dx + j * LANES, LANES)
+            ref[pl.ds(to, LANES), :] = wq[0:turned, pl.ds(at, LANES)].T
+
+    def turn(i, carry):
+        wq_copy(i).wait()
+        turn_into(wt, i, i)
+        return carry
 
     def wo_copy(i):
         span = span_of(base_of(i))
@@ -195,8 +214,10 @@
     second = jnp.max(jnp.where(lane8 == row4 + batch, peak, 0.0), axis=0, keepdims=True)
     stats[me] = jnp.where(lane8[0:1, :] < batch, first, second)
 
-    for i in range(groups):
+    for i in range(2 * groups):
         wq_copy(i).start()
+    early = 1
+    lax.fori_loop(0, early, turn, 0)
 
     pl.semaphore_wait(barrier, n - 1)
 
@@ -217,6 +238,7 @@
     sine = jnp.sin(angle)
     sine = jnp.where(lane8 < HEAD_SIZE // 2, -sine, sine)
 
+    lax.fori_loop(early, 2 * groups - 2, turn, 0)
     all_received(stats, t_send, t_recv)
     if n % 8 == 0:
         rows = [stats[8 * i : 8 * i + 8, 0, :] for i in range(n // 8)]
@@ -242,36 +264,51 @@
     for i in range(groups - 1, -1, -1):
         wo_copy(i).start()
 
-    all_received(xg, x_send, x_recv.at[0], per - 1)
-
-    def project(i, acc):
-        base = base_of(i)
-        wq_copy(i).wait()
-
-        @pl.when(i > 0)
-        def _():
-            all_received(xg, x_send, x_recv.at[i], per)
-
-        for u in range(per):
-            _, ys = gained(base + u)
-            rows = [y * rstd8 / scale8 for y in ys]
-            flat = [row[v * batch : (v + 1) * batch, :] for row in rows for v in range(per8)]
-            span = pl.ds(pl.multiple_of((base + u) * dx, dx), dx)
-            quant[:, span] = jnp.concatenate(flat, axis=1).astype(bf16)
-        span = span_of(base)
-        return acc + lax.dot_general(
-            wq[:, span], quant[:, span], (((1,), (1,)), ((), ())), preferred_element_type=f32
-        )
-
-    acc = lax.fori_loop(0, groups, project, jnp.zeros((cw, batch), f32))
-    proj = (acc.T * token_scale).astype(bf16).astype(f32)
+    def project(i, carry, ref, place):
+        acc, rest = carry
+        for v in range(2):
+            first = half_of(2 * i + v) // dx
+            for u in range(half):
+                _, ys = gained(first + u)
+                rows = [y * rstd8 / scale8 for y in ys]
+                flat = [row[w * batch : (w + 1) * batch, :] for row in rows for w in range(per8)]
+                quant[2 * i + v, :, u * dx : (u + 1) * dx] = jnp.concatenate(
+                    flat, axis=1
+                ).astype(bf16)
+        for v in range(2):
+            x = quant[2 * i + v]
+            to = pl.multiple_of((2 * place + v) * half * dx, half * dx)
+            acc = acc + jnp.dot(x, ref[pl.ds(to, half * dx), :], preferred_element_type=f32)
+            if turned < cw:
+                rest = rest + lax.dot_general(
+                    wq[turned:cw, pl.ds(half_of(2 * i + v), half * dx)],
+                    x,
+                    (((1,), (1,)), ((), ())),
+                    preferred_element_type=f32,
+                )
+        return acc, rest
+
+    def project_middle(i, carry):
+        all_received(xg, x_send, x_recv.at[i], per)
+        return project(i, carry, wt, i)
+
+    carry = (jnp.zeros((batch, turned), f32), jnp.zeros((cw - turned, batch), f32))
+    for i in range(2):
+        wq_copy(2 * groups - 2 + i).wait()
+        all_received(xg, x_send, x_recv.at[i], per if i else per - 1)
+        turn_into(wz, 2 * groups - 2 + i, i)
+        carry = project(i, carry, wt, i)
+    carry = lax.fori_loop(2, groups - 1, project_middle, carry)
+    all_received(xg, x_send, x_recv.at[groups - 1], per)
+    acc, rest = project(groups - 1, carry, wz, 0)
+    if turned < cw:
+        acc = jnp.concatenate([acc, rest.T], axis=1)
+    proj = (acc * token_scale).astype(bf16).astype(f32)
     if padded > cw:
         proj = jnp.concatenate([proj, jnp.zeros((batch, padded - cw), f32)], axis=1)
     if cw % LANES:
         proj = pltpu.roll(proj, lax.rem(me * cw, LANES), 1)
-    for j in range(blocks):
-        stage[j * batch : (j + 1) * batch, :] = proj[:, j * LANES : (j + 1) * LANES]
-    qg[me, 0 : blocks * batch, :] = stage[...].astype(bf16)
+    qg[me] = proj.astype(bf16)
     far_first(lambda k, peer: remote(qg.at[me], qg.at[me], q_send, q_recv, peer).start())
     copy_k.wait()
     copy_v.wait()
@@ -283,68 +320,86 @@
         piece = None
         for d in range(h * LANES // cw, (h * LANES + LANES - 1) // cw + 1):
             block = h - d * cw // LANES
-            part = unpacked[d][block * batch : (block + 1) * batch, :]
+            part = unpacked[d][:, block * LANES : (block + 1) * LANES]
             piece = part if piece is None else piece + part
         heads[h * batch : (h + 1) * batch, :] = piece
 
-    def rotated(rows):
-        count = rows.shape[0]
-        turned = pltpu.roll(rows, HEAD_SIZE // 2, 1)
-        return rows * jnp.tile(cosine, (count // 8, 1)) + turned * jnp.tile(sine, (count // 8, 1))
-
     inv = 1.0 / HEAD_SIZE**0.5
-    rows_g = group * batch
-    cols = batch * positions
-    col = lax.broadcasted_iota(jnp.int32, (8, cols), 1)
-    row = lax.broadcasted_iota(jnp.int32, (8, cols), 0)
-    limit = jnp.zeros((8, cols), jnp.int32)
-    for b in range(batch):
-        limit = jnp.where(col // positions == b, lens_ref[b], limit)
-    valid8 = (row % batch == col // positions) & (me * positions + col % positions < limit)
-    bias8 = jnp.where(valid8, 0.0, -1e30)
-    bias = jnp.tile(bias8, (rows_g // 8, 1))
-    valid = bias == 0.0
-    fresh_rows = rotated(
-        heads[QUERY_HEADS * batch : (QUERY_HEADS + KEY_VALUE_HEADS) * batch, :]
-    )
+
+    def row_of(rows, b):
+        return jnp.broadcast_to(rows[b : b + 1, :], (group, HEAD_SIZE))
+
+    cosines = [row_of(cosine, b) for b in range(batch)]
+    sines = [row_of(sine, b) for b in range(batch)]
+
+    def rotated(rows, cosine, sine):
+        return rows * cosine + pltpu.roll(rows, HEAD_SIZE // 2, 1) * sine
+
+    spot = lax.broadcasted_iota(jnp.int32, (group, positions), 1) + me * positions
+    masks = [jnp.where(spot < lens_ref[b], 0.0, -1e30) for b in range(batch)]
+    units = [(g, b) for g in range(KEY_VALUE_HEADS) for b in range(batch)]
+
+    def stacked(rows):
+        return jnp.concatenate(rows, axis=0)
+
+    valid = stacked([masks[b] for g, b in units]) == 0.0
+    tokens = KEY_VALUE_HEADS * batch
+    first = QUERY_HEADS * batch
+    fresh_k = rotated(
+        heads[first : first + tokens, :],
+        jnp.tile(cosine, (tokens // 8, 1)),
+        jnp.tile(sine, (tokens // 8, 1)),
+    )
+    fresh_v = heads[first + tokens : first + 2 * tokens, :]
+    queries, scores = [], []
+    for g, b in units:
+        q = heads[pl.ds(g * group * batch + b, group, stride=batch), :]
+        q = rotated(q, cosines[b], sines[b]).astype(bf16)
+        k_rows = kv[b, :, g * HEAD_SIZE : (g + 1) * HEAD_SIZE]
+        queries.append(q)
+        scores.append(
+            lax.dot_general(q, k_rows, (((1,), (1,)), ((), ())), preferred_element_type=f32)
+        )
+    s = stacked(scores) * inv
+    top = jnp.max(jnp.where(valid, s, -1e30), axis=-1, keepdims=True)
+    w = jnp.where(valid, jnp.exp(s - top), 0.0)
+    total = jnp.sum(w, axis=-1, keepdims=True)
+    w = w.astype(bf16)
+    o = stacked(
+        [
+            jnp.dot(
+                w[i * group : (i + 1) * group, :],
+                vv[b, :, g * HEAD_SIZE : (g + 1) * HEAD_SIZE],
+                preferred_element_type=f32,
+            )
+            for i, (g, b) in enumerate(units)
+        ]
+    )
+    k_new = stacked([row_of(fresh_k, g * batch + b) for g, b in units])
+    v_new = stacked([row_of(fresh_v, g * batch + b) for g, b in units])
+    s_new = jnp.sum(stacked(queries).astype(f32) * k_new, axis=-1, keepdims=True) * inv
+    s_new = jnp.where(me == 0, s_new, -1e30)
+    top_new = jnp.maximum(top, s_new)
+    keep = jnp.exp(top - top_new)
+    fresh = jnp.where(me == 0, jnp.exp(s_new - top_new), 0.0)
+    total = total * keep + fresh
+    o = o * keep + fresh * v_new
+    some = total > 0.0
+    safe = jnp.where(some, total, 1.0)
+    o = o / safe
+    lse = jnp.where(some, top_new + jnp.log(safe), -1e30)
+    lse = jnp.broadcast_to(lse, o.shape)
+    for i, (g, b) in enumerate(units):
+        spread = pl.ds(g * group * batch + b, group, stride=batch)
+        ordered[0, spread, :] = o[i * group : (i + 1) * group, :]
+        ordered[1, spread, :] = lse[i * group : (i + 1) * group, :]
     own_lane = lax.broadcasted_iota(jnp.int32, (own_rows, LANES), 1)
     own_row = lax.broadcasted_iota(jnp.int32, (own_rows, LANES), 0)
     diagonal = own_lane == own_row
-    for g in range(KEY_VALUE_HEADS):
-        q = rotated(heads[g * rows_g : (g + 1) * rows_g, :]).astype(bf16)
-        k_rows = kv[:, :, g * HEAD_SIZE : (g + 1) * HEAD_SIZE].reshape(cols, HEAD_SIZE)
-        v_rows = vv[:, :, g * HEAD_SIZE : (g + 1) * HEAD_SIZE].reshape(cols, HEAD_SIZE)
-        s = (
-            lax.dot_general(q, k_rows, (((1,), (1,)), ((), ())), preferred_element_type=f32) * inv
-        )
-        top = jnp.max(jnp.where(valid, s, -1e30), axis=-1, keepdims=True)
-        w = jnp.where(valid, jnp.exp(s - top), 0.0)
-        total = jnp.sum(w, axis=-1, keepdims=True)
-        o = jnp.dot(w.astype(bf16), v_rows, preferred_element_type=f32)
-        k_new = fresh_rows[g * batch : (g + 1) * batch, :]
-        base = (QUERY_HEADS + KEY_VALUE_HEADS + g) * batch
-        v_new = heads[base : base + batch, :]
-        s_new = (
-            jnp.sum(q.astype(f32) * jnp.tile(k_new, (group, 1)), axis=-1, keepdims=True) * inv
-        )
-        s_new = jnp.where(me == 0, s_new, -1e30)
-        top_new = jnp.maximum(top, s_new)
-        keep = jnp.exp(top - top_new)
-        fresh = jnp.where(me == 0, jnp.exp(s_new - top_new), 0.0)
-        total = total * keep + fresh
-        o = o * keep + fresh * jnp.tile(v_new, (group, 1))
-        some = total > 0.0
-        safe = jnp.where(some, total, 1.0)
-        o = (o / safe).astype(bf16)
-        lse = jnp.where(some, top_new + jnp.log(safe), -1e30)
-        for j in range(group // own_heads):
-            e = g * (group // own_heads) + j
-            so[e] = o[j * own_rows : (j + 1) * own_rows, :]
-            sl[e] = jnp.sum(
-                jnp.where(diagonal, lse[j * own_rows : (j + 1) * own_rows, :], 0.0),
-                axis=0,
-                keepdims=True,
-            )
+    for e in range(n):
+        rows = slice(e * own_rows, (e + 1) * own_rows)
+        so[e] = ordered[0, rows, :].astype(bf16)
+        sl[e] = jnp.sum(jnp.where(diagonal, ordered[1, rows, :], 0.0), axis=0, keepdims=True)
 
     def send_o(k, peer):
         remote(so.at[peer], og.at[me], o_send, o_recv, peer).start()
@@ -383,25 +438,26 @@
         rs_send[peer] = rows_of(part).astype(bf16)
         remote(rs_send.at[peer], rs_recv.at[me], r_send, r_recv, peer).start()
 
+    def out_of(peer, count):
+        span = pl.ds(pl.multiple_of(peer * dx, dx), count * dx)
+        return jnp.dot(att, wo[:, span], preferred_element_type=f32)
+
     def project_out(j, carry):
-        i = groups - 1 - j
-        base = base_of(i)
-        parts = jnp.dot(att, wo[:, span_of(base)], preferred_element_type=f32)
+        first = base_of(groups - 1 - j)
+        part = out_of(first, per)
         for u in range(per):
-            send_part(base + u, parts[:, u * dx : (u + 1) * dx])
+            send_part(first + u, part[:, u * dx : (u + 1) * dx])
         return carry
 
-    lax.fori_loop(0, groups - 1, project_out, 0)
-
-    def out_of(peer):
-        span = pl.ds(pl.multiple_of(peer * dx, dx), dx)
-        return jnp.dot(att, wo[:, span], preferred_element_type=f32)
-
-    near = [partner(me, k, n) for k in range(per - 1, 0, -1)]
-    parts = [out_of(peer) for peer in near]
-    for peer, part in zip(near, parts):
-        send_part(peer, part)
-    own = rows_of(out_of(me))
+    lax.fori_loop(0, groups - 2, project_out, 0)
+    near = [(base_of(1), per), (half_of(1) // dx, half)]
+    parts = [(first, count, out_of(first, count)) for first, count in near]
+    for first, count, part in parts:
+        for u in range(count):
+            send_part(first + u, part[:, u * dx : (u + 1) * dx])
+    mate = partner(me, 1, n)
+    part, own = out_of(mate, 1), rows_of(out_of(me, 1))
+    send_part(mate, part)
 
     all_received(rs_recv, r_send, r_recv)
     total = own
@@ -448,22 +504,24 @@
     out, token_scale = pl.pallas_call(
         functools.partial(kernel, n),
         out_shape=(
-            jax.ShapeDtypeStruct((pieces * batch, LANES), bf16),
-            jax.ShapeDtypeStruct((1, batch), f32),
+            pltpu.VMEM((pieces * batch, LANES), bf16),
+            pltpu.VMEM((1, batch), f32),
         ),
         in_specs=[hbm] * 9,
         out_specs=(vmem, vmem),
         scratch_shapes=[
             pltpu.VMEM((n, x_height, LANES), bf16),
-            pltpu.VMEM((batch, n * dx), bf16),
+            pltpu.VMEM((n // 2, batch, 2 * dx), bf16),
             pltpu.VMEM((cw, n * dx), bf16),
+            pltpu.VMEM(((n - 4) * dx, cw // LANES * LANES), bf16),
+            pltpu.VMEM((4 * dx, cw // LANES * LANES), bf16),
             pltpu.VMEM((w_out.shape[0], n * dx), bf16),
             pltpu.VMEM(key_cache.shape, bf16),
             pltpu.VMEM(value_cache.shape, bf16),
             pltpu.VMEM((n, 1, LANES), f32),
-            pltpu.VMEM((blocks * batch, LANES), f32),
-            pltpu.VMEM((n, rounded_up(blocks * batch, 8), LANES), bf16),
+            pltpu.VMEM((n, batch, blocks * LANES), bf16),
             pltpu.VMEM((total_heads * batch, HEAD_SIZE), f32),
+            pltpu.VMEM((2, QUERY_HEADS * batch, HEAD_SIZE), f32),
             pltpu.VMEM((n, own_rows, LANES), bf16),
             pltpu.VMEM((n, own_rows, LANES), bf16),
             pltpu.VMEM((n, 1, LANES), f32),
@@ -474,7 +532,7 @@
             pltpu.SMEM((batch,), jnp.int32),
             pltpu.VMEM((1, LANES), f32),
             dma((5,)),
-            dma((n // 4,)),
+            dma((n // 2,)),
             dma((n // 4,)),
             dma((2,)),
             dma(()),
@@ -498,6 +556,8 @@
         positions,
         freq,
     )
+    out = pltpu.with_memory_space_constraint(out, pltpu.VMEM)
+    token_scale = pltpu.with_memory_space_constraint(token_scale, pltpu.VMEM)
     out, token_scale = pl.pallas_call(
         hand_over,
         out_shape=(

time: 34.9 us -> 30.7 us (0.88)
  Pallas kernels: 33.9 us -> 29.9 us
    pallas_call x1, Pallas kernels: 32.6 us -> 29.3 us  [on_device(): pl.pallas_call(functools.partial(kernel, n), out_shape=(pltpu.VMEM((piece...]
    pallas_call x1, Pallas kernels: 1.3 us -> 0.6 us  [on_device(): pl.pallas_call(hand_over, out_shape=(jax.ShapeDtypeStruct(out.shape, out....]
where the time goes in v2:
time: 30.7 us; the launch traced here: 30.5 us
  Pallas kernels  29.9 us (97%)
  between operations  0.64 us (2%)
    pallas_call x1, Pallas kernels, on_device(): pl.pallas_call(functools.partial(kernel, n), out_shape=(pltpu.VMEM((piece...  29.3 us

profile of v2, /device:TPU:0, one launch (start us, length us, event | category | flops | bytes accessed | tf_op | source)
XLA Modules:
  0.0 30.5 jit_solution(15947972832646805117)
XLA Ops:
  0.6 29.3 %decode.1 = (bf16[32,128]{1,0:T(8,128)(2,1)S(1)}, f32[1,4]{1,0:T(1,128)S(1)}) custom-call(bf16[32,128]{1,0:T(8,128)(2,1)} %bitcast.14, bf16[8,128]{1,0:T(8,128)(2,1)} %bitcast.15, bf16[576,16384]{1,0:T(8,128)(2,1)} %bitcast.13, bf16[512,16384]{1,0:T(8,128)(2,1)} %wo_hbm.1, bf16[4,128,512]{2,1,0:T(8,128)(2,1)} %key_hbm.1, bf16[4,128,512]{2,1,0:T(8,128)(2,1)} %value_hbm.1, ...), custom_call_target="tpu_custom_call" | custom-call | tf_op jit(solution)/shard_map/decode/pallas_call | solution.py:504
  29.9 0.6 %hand_over.1 = (bf16[32,128]{1,0:T(8,128)(2,1)}, f32[1,4]{1,0:T(1,128)}) custom-call(bf16[32,128]{1,0:T(8,128)(2,1)S(1)} %get-tuple-element.6.result_ref, f32[1,4]{1,0:T(1,128)S(1)} %get-tuple-element.7.scale_ref), custom_call_target="tpu_custom_call" | custom-call | tf_op jit(solution)/shard_map/hand_over/pallas_call | solution.py:561

commit v3 on v2

--- a/solution.py
+++ b/solution.py
@@ -141,8 +141,21 @@
             device_id_type=pl.DeviceIdType.MESH,
         )
 
+    def far_group(j):
+        if groups != 4:
+            return groups - 1 - j
+        middle = (me // per + me // (2 * per)) % 2
+        return [3 - middle, 2 + middle, 1, 0][j]
+
     def far_first(act):
-        if unrolled:
+        if unrolled and groups == 4:
+            for j in range(groups):
+                for u in range(per - 1, -1, -1):
+                    if j == groups - 1 and u == 0:
+                        continue
+                    k = far_group(j) * per + u
+                    act(k, partner(me, k, n))
+        elif unrolled:
             for k in range(n - 1, 0, -1):
                 act(k, partner(me, k, n))
         else:
@@ -152,6 +165,18 @@
                 return carry
 
             lax.fori_loop(0, n - 1, step, 0)
+
+    def near_first(act):
+        if unrolled:
+            for k in range(1, n):
+                act(k, partner(me, k, n))
+        else:
+
+            def step(k, carry):
+                act(k, partner(me, k, n))
+                return carry
+
+            lax.fori_loop(1, n, step, 0)
 
     def all_sent(ref, send, recv):
         part = ref.at[pl.ds(0, n - 1)]
@@ -175,11 +200,16 @@
         copy.start()
 
     barrier = pltpu.get_barrier_semaphore()
-    far_first(
-        lambda k, peer: pl.semaphore_signal(
+    def announce(peer):
+        pl.semaphore_signal(
             barrier, inc=1, device_id={"tp": peer}, device_id_type=pl.DeviceIdType.MESH
         )
-    )
+
+    if unrolled:
+        for k in range(n - 1, 0, -1):
+            announce(partner(me, k, n))
+    else:
+        far_first(lambda k, peer: announce(peer))
     copy_k = pltpu.make_async_copy(key_hbm, kv, kv_sem.at[0])
     copy_v = pltpu.make_async_copy(value_hbm, vv, kv_sem.at[1])
 
@@ -216,17 +246,16 @@
 
     for i in range(2 * groups):
         wq_copy(i).start()
-    early = 1
-    lax.fori_loop(0, early, turn, 0)
 
     pl.semaphore_wait(barrier, n - 1)
 
     far_first(
         lambda k, peer: remote(stats.at[me], stats.at[me], t_send, t_recv, peer).start()
     )
-    far_first(
-        lambda k, peer: remote(xg.at[me], xg.at[me], x_send, x_recv.at[k // per], peer).start()
-    )
+    def send_x(k, peer):
+        remote(xg.at[me], xg.at[me], x_send, x_recv.at[k // per], peer).start()
+
+    near_first(send_x)
 
     for copy in small[2:]:
         copy.wait()
@@ -238,7 +267,7 @@
     sine = jnp.sin(angle)
     sine = jnp.where(lane8 < HEAD_SIZE // 2, -sine, sine)
 
-    lax.fori_loop(early, 2 * groups - 2, turn, 0)
+    lax.fori_loop(0, 2 * groups - 2, turn, 0)
     all_received(stats, t_send, t_recv)
     if n % 8 == 0:
         rows = [stats[8 * i : 8 * i + 8, 0, :] for i in range(n // 8)]
@@ -442,14 +471,21 @@
         span = pl.ds(pl.multiple_of(peer * dx, dx), count * dx)
         return jnp.dot(att, wo[:, span], preferred_element_type=f32)
 
-    def project_out(j, carry):
-        first = base_of(groups - 1 - j)
+    def project_out(i):
+        first = base_of(i)
         part = out_of(first, per)
         for u in range(per):
             send_part(first + u, part[:, u * dx : (u + 1) * dx])
+
+    def project_far(j, carry):
+        if groups == 4:
+            middle = (me // per + me // (2 * per)) % 2
+            project_out(3 - j - middle * (1 - 2 * j))
+        else:
+            project_out(groups - 1 - j)
         return carry
 
-    lax.fori_loop(0, groups - 2, project_out, 0)
+    lax.fori_loop(0, groups - 2, project_far, 0)
     near = [(base_of(1), per), (half_of(1) // dx, half)]
     parts = [(first, count, out_of(first, count)) for first, count in near]
     for first, count, part in parts:

time: 30.7 us -> 30 us (0.977)
  Pallas kernels: 29.9 us -> 29.1 us
    pallas_call x1, Pallas kernels: 29.3 us -> 28.5 us  [on_device(): pl.pallas_call(functools.partial(kernel, n), out_shape=(pltpu.VMEM((piece...]
where the time goes in v3:
time: 30 us; the launch traced here: 29.7 us
  Pallas kernels  29.1 us (97%)
  between operations  0.64 us (2%)
    pallas_call x1, Pallas kernels, on_device(): pl.pallas_call(functools.partial(kernel, n), out_shape=(pltpu.VMEM((piece...  28.5 us
    pallas_call x1, Pallas kernels, on_device(): pl.pallas_call(hand_over, out_shape=(jax.ShapeDtypeStruct(out.shape, out....  0.6 us

profile of v3, /device:TPU:0, one launch (start us, length us, event | category | flops | bytes accessed | tf_op | source)
XLA Modules:
  0.0 29.7 jit_solution(1723650411140875794)
XLA Ops:
  0.6 28.5 %decode.1 = (bf16[32,128]{1,0:T(8,128)(2,1)S(1)}, f32[1,4]{1,0:T(1,128)S(1)}) custom-call(bf16[32,128]{1,0:T(8,128)(2,1)} %bitcast.14, bf16[8,128]{1,0:T(8,128)(2,1)} %bitcast.15, bf16[576,16384]{1,0:T(8,128)(2,1)} %bitcast.13, bf16[512,16384]{1,0:T(8,128)(2,1)} %wo_hbm.1, bf16[4,128,512]{2,1,0:T(8,128)(2,1)} %key_hbm.1, bf16[4,128,512]{2,1,0:T(8,128)(2,1)} %value_hbm.1, ...), custom_call_target="tpu_custom_call" | custom-call | tf_op jit(solution)/shard_map/decode/pallas_call | solution.py:540
  29.1 0.6 %hand_over.1 = (bf16[32,128]{1,0:T(8,128)(2,1)}, f32[1,4]{1,0:T(1,128)}) custom-call(bf16[32,128]{1,0:T(8,128)(2,1)S(1)} %get-tuple-element.6.result_ref, f32[1,4]{1,0:T(1,128)S(1)} %get-tuple-element.7.scale_ref), custom_call_target="tpu_custom_call" | custom-call | tf_op jit(solution)/shard_map/hand_over/pallas_call | solution.py:597

commit v4 on v3

--- a/solution.py
+++ b/solution.py
@@ -52,6 +52,7 @@
     wz,
     wo,
     kv,
+    kt,
     vv,
     stats,
     qg,
@@ -213,6 +214,8 @@
     copy_k = pltpu.make_async_copy(key_hbm, kv, kv_sem.at[0])
     copy_v = pltpu.make_async_copy(value_hbm, vv, kv_sem.at[1])
 
+    for i in range(2 * groups):
+        wq_copy(i).start()
     small[0].wait()
     small[1].wait()
 
@@ -244,8 +247,6 @@
     second = jnp.max(jnp.where(lane8 == row4 + batch, peak, 0.0), axis=0, keepdims=True)
     stats[me] = jnp.where(lane8[0:1, :] < batch, first, second)
 
-    for i in range(2 * groups):
-        wq_copy(i).start()
 
     pl.semaphore_wait(barrier, n - 1)
 
@@ -256,16 +257,6 @@
         remote(xg.at[me], xg.at[me], x_send, x_recv.at[k // per], peer).start()
 
     near_first(send_x)
-
-    for copy in small[2:]:
-        copy.wait()
-    place = jnp.zeros((8, LANES), f32)
-    for b in range(batch):
-        place = jnp.where(row4 == b, pos_ref[b].astype(f32), place)
-    angle = place * freq_ref[...]
-    cosine = jnp.cos(angle)
-    sine = jnp.sin(angle)
-    sine = jnp.where(lane8 < HEAD_SIZE // 2, -sine, sine)
 
     lax.fori_loop(0, 2 * groups - 2, turn, 0)
     all_received(stats, t_send, t_recv)
@@ -310,8 +301,8 @@
             acc = acc + jnp.dot(x, ref[pl.ds(to, half * dx), :], preferred_element_type=f32)
             if turned < cw:
                 rest = rest + lax.dot_general(
+                    x,
                     wq[turned:cw, pl.ds(half_of(2 * i + v), half * dx)],
-                    x,
                     (((1,), (1,)), ((), ())),
                     preferred_element_type=f32,
                 )
@@ -321,7 +312,7 @@
         all_received(xg, x_send, x_recv.at[i], per)
         return project(i, carry, wt, i)
 
-    carry = (jnp.zeros((batch, turned), f32), jnp.zeros((cw - turned, batch), f32))
+    carry = (jnp.zeros((batch, turned), f32), jnp.zeros((batch, cw - turned), f32))
     for i in range(2):
         wq_copy(2 * groups - 2 + i).wait()
         all_received(xg, x_send, x_recv.at[i], per if i else per - 1)
@@ -331,7 +322,7 @@
     all_received(xg, x_send, x_recv.at[groups - 1], per)
     acc, rest = project(groups - 1, carry, wz, 0)
     if turned < cw:
-        acc = jnp.concatenate([acc, rest.T], axis=1)
+        acc = jnp.concatenate([acc, rest], axis=1)
     proj = (acc * token_scale).astype(bf16).astype(f32)
     if padded > cw:
         proj = jnp.concatenate([proj, jnp.zeros((batch, padded - cw), f32)], axis=1)
@@ -339,8 +330,20 @@
         proj = pltpu.roll(proj, lax.rem(me * cw, LANES), 1)
     qg[me] = proj.astype(bf16)
     far_first(lambda k, peer: remote(qg.at[me], qg.at[me], q_send, q_recv, peer).start())
+    for copy in small[2:]:
+        copy.wait()
+    place = jnp.zeros((8, LANES), f32)
+    for b in range(batch):
+        place = jnp.where(row4 == b, pos_ref[b].astype(f32), place)
+    angle = place * freq_ref[...]
+    cosine = jnp.cos(angle)
+    sine = jnp.sin(angle)
+    sine = jnp.where(lane8 < HEAD_SIZE // 2, -sine, sine)
+
     copy_k.wait()
     copy_v.wait()
+    for b in range(batch):
+        kt[b] = kv[b].T
     all_received(qg, q_send, q_recv)
 
     total_heads = QUERY_HEADS + 2 * KEY_VALUE_HEADS
@@ -384,11 +387,9 @@
     for g, b in units:
         q = heads[pl.ds(g * group * batch + b, group, stride=batch), :]
         q = rotated(q, cosines[b], sines[b]).astype(bf16)
-        k_rows = kv[b, :, g * HEAD_SIZE : (g + 1) * HEAD_SIZE]
+        keys = kt[b, g * HEAD_SIZE : (g + 1) * HEAD_SIZE, :]
         queries.append(q)
-        scores.append(
-            lax.dot_general(q, k_rows, (((1,), (1,)), ((), ())), preferred_element_type=f32)
-        )
+        scores.append(jnp.dot(q, keys, preferred_element_type=f32))
     s = stacked(scores) * inv
     top = jnp.max(jnp.where(valid, s, -1e30), axis=-1, keepdims=True)
     w = jnp.where(valid, jnp.exp(s - top), 0.0)
@@ -553,6 +554,7 @@
             pltpu.VMEM((4 * dx, cw // LANES * LANES), bf16),
             pltpu.VMEM((w_out.shape[0], n * dx), bf16),
             pltpu.VMEM(key_cache.shape, bf16),
+            pltpu.VMEM((batch, key_cache.shape[2], key_cache.shape[1]), bf16),
             pltpu.VMEM(value_cache.shape, bf16),
             pltpu.VMEM((n, 1, LANES), f32),
             pltpu.VMEM((n, batch, blocks * LANES), bf16),

time: 30 us -> 29.6 us (0.987)
  Pallas kernels: 29.1 us -> 28.7 us
    pallas_call x1, Pallas kernels: 28.5 us -> 28.1 us  [on_device(): pl.pallas_call(functools.partial(kernel, n), out_shape=(pltpu.VMEM((piece...]
where the time goes in v4:
time: 29.6 us; the launch traced here: 29.4 us
  Pallas kernels  28.7 us (97%)
  between operations  0.64 us (2%)
    pallas_call x1, Pallas kernels, on_device(): pl.pallas_call(functools.partial(kernel, n), out_shape=(pltpu.VMEM((piece...  28.1 us
    pallas_call x1, Pallas kernels, on_device(): pl.pallas_call(hand_over, out_shape=(jax.ShapeDtypeStruct(out.shape, out....  0.6 us

profile of v4, /device:TPU:0, one launch (start us, length us, event | category | flops | bytes accessed | tf_op | source)
XLA Modules:
  0.0 29.4 jit_solution(16464340625426427221)
XLA Ops:
  0.6 28.1 %decode.1 = (bf16[32,128]{1,0:T(8,128)(2,1)S(1)}, f32[1,4]{1,0:T(1,128)S(1)}) custom-call(bf16[32,128]{1,0:T(8,128)(2,1)} %bitcast.14, bf16[8,128]{1,0:T(8,128)(2,1)} %bitcast.15, bf16[576,16384]{1,0:T(8,128)(2,1)} %bitcast.13, bf16[512,16384]{1,0:T(8,128)(2,1)} %wo_hbm.1, bf16[4,128,512]{2,1,0:T(8,128)(2,1)} %key_hbm.1, bf16[4,128,512]{2,1,0:T(8,128)(2,1)} %value_hbm.1, ...), custom_call_target="tpu_custom_call" | custom-call | tf_op jit(solution)/shard_map/decode/pallas_call | solution.py:541
  28.8 0.6 %hand_over.1 = (bf16[32,128]{1,0:T(8,128)(2,1)}, f32[1,4]{1,0:T(1,128)}) custom-call(bf16[32,128]{1,0:T(8,128)(2,1)S(1)} %get-tuple-element.6.result_ref, f32[1,4]{1,0:T(1,128)S(1)} %get-tuple-element.7.scale_ref), custom_call_target="tpu_custom_call" | custom-call | tf_op jit(solution)/shard_map/hand_over/pallas_call | solution.py:599

commit v5 on v4

--- a/solution.py
+++ b/solution.py
@@ -123,14 +123,19 @@
             to = pl.multiple_of(place * half * dx + j * LANES, LANES)
             ref[pl.ds(to, LANES), :] = wq[0:turned, pl.ds(at, LANES)].T
 
-    def turn(i, carry):
-        wq_copy(i).wait()
-        turn_into(wt, i, i)
+    def turn(i, count):
+        for v in range(count):
+            wq_copy(i + v).wait()
+        for v in range(count):
+            turn_into(wt, i + v, i + v)
+
+    def turn_two(j, carry):
+        turn(2 * j + 2, 2)
         return carry
 
     def wo_copy(i):
         span = span_of(base_of(i))
-        return pltpu.make_async_copy(wo_hbm.at[:, span], wo.at[:, span], wo_sem.at[i])
+        return pltpu.make_async_copy(wo_hbm.at[:, span], wo.at[:, span], wo_sem)
 
     def remote(src, dst, send, recv, peer):
         return pltpu.make_async_remote_copy(
@@ -258,7 +263,9 @@
 
     near_first(send_x)
 
-    lax.fori_loop(0, 2 * groups - 2, turn, 0)
+    turn(0, 1)
+    turn(1, 1)
+    lax.fori_loop(0, groups - 2, turn_two, 0)
     all_received(stats, t_send, t_recv)
     if n % 8 == 0:
         rows = [stats[8 * i : 8 * i + 8, 0, :] for i in range(n // 8)]
@@ -316,6 +323,7 @@
     for i in range(2):
         wq_copy(2 * groups - 2 + i).wait()
         all_received(xg, x_send, x_recv.at[i], per if i else per - 1)
+    for i in range(2):
         turn_into(wz, 2 * groups - 2 + i, i)
         carry = project(i, carry, wt, i)
     carry = lax.fori_loop(2, groups - 1, project_middle, carry)
@@ -438,8 +446,7 @@
     far_first(send_o)
     og[me] = so[me]
     lg[me] = sl[me]
-    for i in range(groups):
-        wo_copy(i).wait()
+    pltpu.make_async_copy(wo_hbm, wo, wo_sem).wait()
 
     all_received(lg, l_send, l_recv)
     all_received(og, o_send, o_recv)
@@ -571,7 +578,7 @@
             pltpu.VMEM((1, LANES), f32),
             dma((5,)),
             dma((n // 2,)),
-            dma((n // 4,)),
+            dma(()),
             dma((2,)),
             dma(()),
             dma(()),

time: 29.6 us -> 29.5 us (level)
  no operation moved by 1% of the time
where the time goes in v5:
time: 29.5 us; the launch traced here: 29.3 us
  Pallas kernels  28.7 us (97%)
  between operations  0.64 us (2%)
    pallas_call x1, Pallas kernels, on_device(): pl.pallas_call(functools.partial(kernel, n), out_shape=(pltpu.VMEM((piece...  28 us
    pallas_call x1, Pallas kernels, on_device(): pl.pallas_call(hand_over, out_shape=(jax.ShapeDtypeStruct(out.shape, out....  0.6 us

profile of v5, /device:TPU:0, one launch (start us, length us, event | category | flops | bytes accessed | tf_op | source)
XLA Modules:
  0.0 29.3 jit_solution(12176551755779347556)
XLA Ops:
  0.6 28.0 %decode.1 = (bf16[32,128]{1,0:T(8,128)(2,1)S(1)}, f32[1,4]{1,0:T(1,128)S(1)}) custom-call(bf16[32,128]{1,0:T(8,128)(2,1)} %bitcast.14, bf16[8,128]{1,0:T(8,128)(2,1)} %bitcast.15, bf16[576,16384]{1,0:T(8,128)(2,1)} %bitcast.13, bf16[512,16384]{1,0:T(8,128)(2,1)} %wo_hbm.1, bf16[4,128,512]{2,1,0:T(8,128)(2,1)} %key_hbm.1, bf16[4,128,512]{2,1,0:T(8,128)(2,1)} %value_hbm.1, ...), custom_call_target="tpu_custom_call" | custom-call | tf_op jit(solution)/shard_map/decode/pallas_call | solution.py:548
  28.7 0.6 %hand_over.1 = (bf16[32,128]{1,0:T(8,128)(2,1)}, f32[1,4]{1,0:T(1,128)}) custom-call(bf16[32,128]{1,0:T(8,128)(2,1)S(1)} %get-tuple-element.6.result_ref, f32[1,4]{1,0:T(1,128)S(1)} %get-tuple-element.7.scale_ref), custom_call_target="tpu_custom_call" | custom-call | tf_op jit(solution)/shard_map/hand_over/pallas_call | solution.py:606
